TPU v7x, 32 devices: a whole 2x2x4 slice. The times are simulated.
32 devices in a mesh: dp: 8 (over y, x, core), mp: 4 (over z).
Axes of the slice: x: 2, y: 2, z: 4, core: 2. Of those that a mesh axis runs over, the one named last changes fastest.
Arguments:
- tokens: bfloat16 [12288, 4096], P('dp'), may hold values from -40 to 40
- norm_gain: bfloat16 [4096], replicated, may hold values from 0.099609375 to 1.8984375
- w_query: bfloat16 [4096, 2048], P(None, 'mp'), may hold values from -1 to 1
- w_key: bfloat16 [4096, 512], P(None, 'mp'), may hold values from -4 to 4
- w_value: bfloat16 [4096, 512], P(None, 'mp'), may hold values from -0.09375 to 0.09375
- w_out: bfloat16 [2048, 4096], P('mp'), may hold values from -0.125 to 0.125
- seq_starts: int32 [64], P('dp'), may hold values from 0 to 1408, as said below
- seq_lengths: int32 [64], P('dp'), may hold values from 128 to 640
- episode_ids: int32 [64], replicated, may hold values from 0 to 0, as said below
- class_ids: int32 [64], replicated, may hold values from 0 to 31
- query_flags: int32 [64], replicated, may hold values from 0 to 1
Outputs:
- log_probs: float32 [64, 32], P('dp')
- prototypes: float32 [32, 4096], P(None, 'mp')
Inputs may be any that keep to these rules, and one draw needn't show every extreme that they name: `seq_starts`: slot s lies in the buffer of dp index s // 8; the slots of one buffer are disjoint and in increasing order of start; start plus length is at most 1536, and in every draw the last slot of some buffer ends at row 1536. `episode_ids`: every class of every episode has at least one support sequence.
All inputs are finite; a program needn't handle non-finite values.
Results may differ from a plain program's by a relative error of at most 0.004.
Values sent between devices are 32-bit elements; how exact they have to be, the bound alone decides.
A program may use at most 128 MiB of HBM per device.

v0:
```python
import math

import jax
import jax.numpy as jnp
from jax import lax
from jax.sharding import PartitionSpec as P

HEAD_DIM = 128
WAYS = 32


ROPE_BASE = 500000.0
NEG_FILL = -1e30


def rotate(vectors, positions):
    half_dim = vectors.shape[-1] // 2
    frequency = jnp.power(
        ROPE_BASE, -(jnp.arange(half_dim, dtype=jnp.float32) * 2.0 / vectors.shape[-1])
    )
    angles = positions.astype(jnp.float32)[:, None] * frequency[None, :]
    cosine = jnp.cos(angles)[:, None, :]
    sine_part = jnp.sin(angles)[:, None, :]
    leading = vectors[..., :half_dim]
    trailing = vectors[..., half_dim:]
    return jnp.concatenate(
        [leading * cosine - trailing * sine_part, trailing * cosine + leading * sine_part], axis=-1
    )


def layout_of(starts, lengths, buffer_len):
    token_index = jnp.arange(buffer_len, dtype=jnp.int32)
    inside = (token_index[:, None] >= starts[None, :]) & (
        token_index[:, None] < (starts + lengths)[None, :]
    )
    slot_number = jnp.arange(starts.shape[0], dtype=jnp.int32)
    segment = jnp.sum(jnp.where(inside, slot_number[None, :] + 1, 0), axis=1) - 1
    position = jnp.sum(jnp.where(inside, token_index[:, None] - starts[None, :], 0), axis=1)
    return (segment, position, inside)


def allowed_mask(segment, row_start, row_count, col_count):
    rows_index = row_start + jnp.arange(row_count, dtype=jnp.int32)
    cols_index = jnp.arange(col_count, dtype=jnp.int32)
    seg_rows = segment[row_start : row_start + row_count]
    seg_cols = segment[:col_count]
    same = (
        (seg_rows[:, None] == seg_cols[None, :])
        & (seg_rows[:, None] >= 0)
        & (cols_index[None, :] < rows_index[:, None])
    )
    return (rows_index[:, None] == cols_index[None, :]) | same


def softmax_rows(scores, permitted):
    masked_scores = jnp.where(permitted[None, None], scores, NEG_FILL)
    row_peak = jnp.max(masked_scores, axis=-1, keepdims=True)
    exponent = jnp.exp(masked_scores - row_peak)
    totals = jnp.sum(exponent, axis=-1, keepdims=True)
    return (exponent / totals).astype(jnp.bfloat16)


def pick_block(length_rows):
    for candidate in (512, 384, 256, 128):
        return candidate
    return length_rows


def per_device(
    tokens,
    norm_gain,
    w_query,
    w_key,
    w_value,
    w_out,
    seq_starts,
    seq_lengths,
    episode_ids,
    class_ids,
    query_flags,
):
    buffer_len = tokens.shape[0]
    model_width = tokens.shape[1]
    seq_count = seq_starts.shape[0]
    head_dim = HEAD_DIM
    heads_local = w_query.shape[1] // head_dim
    kv_local = w_key.shape[1] // head_dim
    group_size = heads_local // kv_local
    inv_root = 1.0 / math.sqrt(head_dim)
    highest = lax.Precision.HIGHEST
    segment, position, inside = layout_of(seq_starts, seq_lengths, buffer_len)
    widened = tokens.astype(jnp.float32)
    normed = (
        widened
        * lax.rsqrt(jnp.mean(widened * widened, axis=-1, keepdims=True) + 1e-05)
        * norm_gain.astype(jnp.float32)
    ).astype(jnp.bfloat16)
    queries = rotate(
        jnp.dot(normed, w_query, preferred_element_type=jnp.float32).reshape(
            buffer_len, heads_local, head_dim
        ),
        position,
    ).astype(jnp.bfloat16)
    queries = queries.reshape(buffer_len, kv_local, group_size, head_dim)
    keys_rot = rotate(
        jnp.dot(normed, w_key, preferred_element_type=jnp.float32).reshape(
            buffer_len, kv_local, head_dim
        ),
        position,
    ).astype(jnp.bfloat16)
    values_all = (
        jnp.dot(normed, w_value, preferred_element_type=jnp.float32)
        .astype(jnp.bfloat16)
        .reshape(buffer_len, kv_local, head_dim)
    )
    block_rows = pick_block(buffer_len)
    block_count = buffer_len // block_rows
    mixed_blocks = []
    for query_block in range(block_count):
        row_start = query_block * block_rows
        key_end = row_start + block_rows
        block_queries = queries[row_start:key_end]
        permitted = allowed_mask(segment, row_start, block_rows, key_end)
        scores = (
            jnp.einsum(
                "qngd,knd->ngqk",
                block_queries,
                keys_rot[:key_end],
                preferred_element_type=jnp.float32,
            )
            * inv_root
        )
        attention_probs = softmax_rows(scores, permitted)
        mixed_out = jnp.einsum(
            "ngqk,knd->qngd",
            attention_probs,
            values_all[:key_end],
            preferred_element_type=jnp.float32,
        )
        mixed_blocks.append(
            mixed_out.astype(jnp.bfloat16).reshape(block_rows, heads_local * head_dim)
        )
    attended = jnp.concatenate(mixed_blocks, axis=0)
    member = inside.T.astype(jnp.bfloat16)
    attended_sums = jnp.dot(member, attended, preferred_element_type=jnp.float32)
    token_sums = jnp.dot(member, tokens, preferred_element_type=jnp.float32)
    high_part = attended_sums.astype(jnp.bfloat16)
    low_part = (attended_sums - high_part.astype(jnp.float32)).astype(jnp.bfloat16)
    head_part = jnp.dot(high_part, w_out, preferred_element_type=jnp.float32) + jnp.dot(
        low_part, w_out, preferred_element_type=jnp.float32
    )
    token_counts = seq_lengths.astype(jnp.float32)[:, None]
    mp_size = lax.axis_size("mp")
    mp_rank = lax.axis_index("mp")
    share_cols = model_width // mp_size
    pooled = (token_sums + lax.psum(head_part, "mp")) / token_counts
    embedded = pooled * lax.rsqrt(jnp.mean(pooled * pooled, axis=-1, keepdims=True) + 1e-06)
    seq_total = episode_ids.shape[0]
    episodes = max(1, seq_total // (2 * WAYS))
    classes = episodes * WAYS
    global_class = episode_ids * WAYS + class_ids
    is_support = query_flags == 0
    class_range = jnp.arange(classes, dtype=jnp.int32)
    select_all = ((global_class[None, :] == class_range[:, None]) & is_support[None, :]).astype(
        jnp.float32
    )
    dp_first = lax.axis_index("dp") * seq_count
    class_sums = jnp.dot(
        select_all, lax.all_gather(embedded, "dp", axis=0, tiled=True), precision=highest
    )
    proto_scale = jnp.mean(class_sums * class_sums, axis=-1)
    prototypes = class_sums * lax.rsqrt(proto_scale + 1e-06)[:, None]
    difference = embedded[:, None, :] - prototypes[None, :, :]
    distance = jnp.sum(difference * difference, axis=-1)
    proto_out = lax.dynamic_slice_in_dim(prototypes, mp_rank * share_cols, share_cols, 1)
    own_episode = lax.dynamic_slice_in_dim(episode_ids, dp_first, seq_count, 0)
    own_query = lax.dynamic_slice_in_dim(query_flags, dp_first, seq_count, 0)
    episode_range = jnp.arange(episodes, dtype=jnp.int32)
    picked = jnp.sum(
        jnp.where(
            own_episode[:, None, None] == episode_range[None, :, None],
            distance.reshape(seq_count, episodes, WAYS),
            0.0,
        ),
        axis=1,
    )
    logits = -picked / math.sqrt(model_width)
    row_peak = jnp.max(logits, axis=-1, keepdims=True)
    shifted = logits - row_peak
    log_probs = shifted - jnp.log(jnp.sum(jnp.exp(shifted), axis=-1, keepdims=True))
    log_probs = jnp.where(own_query[:, None] == 1, log_probs, 0.0)
    return (log_probs, proto_out)


def solution(mesh):
    placed = (
        P("dp", None),
        P(),
        P(None, "mp"),
        P(None, "mp"),
        P(None, "mp"),
        P("mp", None),
        P("dp"),
        P("dp"),
        P(),
        P(),
        P(),
    )
    return jax.shard_map(
        per_device,
        mesh=mesh,
        in_specs=placed,
        out_specs=(P("dp", None), P(None, "mp")),
        check_vma=False,
    )
```

profile of v0, /device:TPU:0, one launch (start us, length us, event | category | flops | bytes accessed | tf_op | source)
XLA Modules:
  0.0 166.5 jit_solution(195916968314349228)
XLA Ops:
  7.2 0.0 copy-start
  7.2 0.0 all-reduce.2.cloned.1.call-start
  7.3 0.8 fusion.86
  8.0 0.8 select_reduce_fusion.1
  8.8 0.0 copy-start.3
  8.8 0.0 copy-start.6
  8.9 7.1 %fusion = f32[1536]{0:T(1024)S(1)} fusion(bf16[1536,4096]{1,0:T(8,128)(2,1)} %param.11), kind=kLoop, calls=%fused_computation.2 | loop fusion | flops 18872832 | bytes 12589056 | tf_op jit(solution)/shard_map/reduce_sum | solution.py:95
  15.9 0.0 copy-done.3
  15.9 0.0 copy-done.6
  16.0 7.9 %fusion.2 = bf16[1536,4096]{1,0:T(8,128)(2,1)S(1)} fusion(bf16[1536,4096]{1,0:T(8,128)(2,1)} %param.11, f32[4096]{0:T(1024)S(1)} %convert_element_type.82, f32[1536]{0:T(1024)S(1)} %add_rsqrt_fusion), kind=kLoop, calls=%fused_computation.4 | loop fusion | flops 25165824 | bytes 25188352 | tf_op jit(solution)/shard_map/convert_element_type | solution.py:97
  23.9 0.0 copy-done
  23.9 3.4 %convolution_convert_fusion = bf16[1536,128]{1,0:T(8,128)(2,1)S(1)} fusion(bf16[1536,4096]{1,0:T(8,128)(2,1)S(1)} %fusion.2, bf16[4096,128]{1,0:T(8,128)(2,1)S(1)} %copy-done), kind=kOutput, calls=%fused_computation.35 | convolution fusion | flops 1610809344 | bytes 14024704 | tf_op jit(solution)/shard_map/dot_general | solution.py:112
  27.3 5.5 %convolution_bitcast_fusion = f32[1536,1,128]{0,2,1:T(8,128)S(1)} fusion(bf16[1536,4096]{1,0:T(8,128)(2,1)S(1)} %fusion.2, bf16[4096,128]{1,0:T(8,128)(2,1)} %param.14), kind=kOutput, calls=%fused_computation.34 | convolution fusion | flops 1610612736 | bytes 14417920 | tf_op jit(solution)/shard_map/dot_general | solution.py:106
  32.9 9.7 %fusion.87 = f32[1536,512]{0,1:T(8,128)} fusion(bf16[1536,4096]{1,0:T(8,128)(2,1)S(1)} %fusion.2, bf16[4096,512]{1,0:T(8,128)(2,1)} %param.13), kind=kOutput, calls=%fused_computation.142 | convolution fusion | flops 6442450944 | bytes 19922944 | tf_op jit(solution)/shard_map/dot_general | solution.py:99
  42.5 4.3 %multiply_cosine_fusion = (f32[1536,64]{1,0:T(8,128)}, f32[1536,64]{1,0:T(8,128)}) fusion(f32[64]{0:T(128)S(1)} %negate_power_fusion, f32[1536]{0:T(1024)S(1)} %convert_element_type.85), kind=kLoop, calls=%fused_computation.57 | loop fusion | flops 98304 | bytes 792832 | tf_op jit(solution)/shard_map/cos | solution.py:22
  46.8 1.6 fusion.51
  48.4 3.3 %fusion.84 = (f32[1536,4,64]{0,2,1:T(8,128)}, f32[1536,4,64]{0,2,1:T(8,128)S(1)}) fusion(f32[1536,4,128]{0,2,1:T(8,128)} %bitcast.120), kind=kLoop, calls=%fused_computation.139 | loop fusion | bytes 6291456 | tf_op jit(solution)/shard_map/slice | solution.py:25
  51.7 3.3 %copy.51 = f32[1536,4,64]{2,0,1:T(8,128)} copy(f32[1536,4,64]{0,2,1:T(8,128)} %get-tuple-element.6) | data formatting | bytes 3145728
  55.0 2.3 %copy.50 = f32[1536,4,64]{2,0,1:T(8,128)} copy(f32[1536,4,64]{0,2,1:T(8,128)S(1)} %get-tuple-element.7) | data formatting | bytes 3145728
  57.3 0.3 fusion.36
  57.6 0.0 slice-done
  57.6 0.8 fusion.18
  58.4 4.0 %subtract_convert_fusion = (bf16[1536,4,64]{2,0,1:T(8,128)(2,1)S(1)}, bf16[1536,4,64]{2,0,1:T(8,128)(2,1)S(1)}) fusion(f32[1536,4,64]{2,0,1:T(8,128)} %copy.51, f32[1536,4,64]{2,0,1:T(8,128)} %copy.50, f32[1536,64]{1,0:T(8,128)} %get-tuple-element.11, f32[1536,64]{1,0:T(8,128)} %get-tuple-element.10), kind=kLoop, calls=%fused_computation.31 | loop fusion | flops 3145728 | bytes 5505024 | tf_op jit(solution)/shard_map/convert.4
  62.4 1.2 fusion.13
  63.6 2.0 %fusion.6 = (f32[4,512]{1,0:T(4,128)S(1)}, f32[1024,512,4]{1,0,2:T(8,128)S(1)}) fusion(pred[512,1024]{0,1:T(8,128)(4,1)S(1)} %fusion.18, bf16[1536,4,64]{2,0,1:T(8,128)(2,1)S(1)} %get-tuple-element.4, bf16[1536,4,64]{2,0,1:T(8,128)(2,1)S(1)} %get-tuple-element.5, bf16[1536,1,64]{0,2,1:T(8,128)(2,1)S(1)} %get-tuple-element.9, ...), kind=kOutput, calls=%fused_computation.14 | convolution fusion | flops 544733184 | bytes 10887168 | tf_op jit(solution)/shard_map/qngd,knd->ngqk/dot_general | solution.py:125
  65.7 0.9 fusion.12
  66.6 1.5 fusion.30
  68.0 1.9 %fusion.5 = f32[4,512]{1,0:T(4,128)S(1)} fusion(f32[1024,512,4]{1,0,2:T(8,128)S(1)} %get-tuple-element.23, f32[4,512]{1,0:T(4,128)S(1)} %get-tuple-element.22, pred[512,1024]{0,1:T(8,128)(4,1)S(1)} %fusion.18), kind=kLoop, calls=%fused_computation.13 | loop fusion | flops 8386560 | bytes 8929280 | tf_op jit(solution)/shard_map/reduce_sum | solution.py:59
  69.9 0.0 copy-start.4
  69.9 2.7 %fusion.27 = bf16[128,4,512]{2,0,1:T(8,128)(2,1)S(1)} fusion(f32[4,512]{1,0:T(4,128)S(1)} %fusion.5, f32[4,512]{1,0:T(4,128)S(1)} %get-tuple-element.22, f32[1024,512,4]{1,0,2:T(8,128)S(1)} %get-tuple-element.23, pred[512,1024]{0,1:T(8,128)(4,1)S(1)} %fusion.18, bf16[1536,128]{1,0:T(8,128)(2,1)S(1)} %convolution_convert_fusion), kind=kOutput, calls=%fused_computation.53 | convolution fusion | flops 547618816 | bytes 9715712 | tf_op jit(solution)/shard_map/ngqk,knd->qngd/dot_general | solution.py:134
  72.6 0.0 copy-done.4
  72.6 1.7 %fusion.14 = pred[512,1536]{0,1:T(8,128)(4,1)S(1)} fusion(s32[512]{0:T(512)S(1)} %get-tuple-element.16, s32[512]{0:T(512)S(1)} %iota_add_fusion, s32[1536]{0:T(1024)S(1)} %copy-done.4, pred[512]{0:T(512)(128)(4,1)S(1)} %get-tuple-element.14), kind=kLoop, calls=%fused_computation.32 | loop fusion | flops 4718592 | bytes 797184 | tf_op jit(solution)/shard_map/or | solution.py:52
  74.4 2.8 %fusion.4 = (f32[4,512]{1,0:T(4,128)S(1)}, f32[1536,512,4]{1,0,2:T(8,128)S(1)}) fusion(pred[512,1536]{0,1:T(8,128)(4,1)S(1)} %fusion.14, bf16[1536,4,64]{2,0,1:T(8,128)(2,1)S(1)} %get-tuple-element.5, bf16[1536,4,64]{2,0,1:T(8,128)(2,1)S(1)} %get-tuple-element.4, bf16[1536,64]{0,1:T(8,128)(2,1)S(1)} %bitcast.119, bf16[1536,64]{0,1:T(8,128)(2,1)S(1)} %bitcast.118), kind=kOutput, calls=%fused_computation.9 | convolution fusion | flops 816576512 | bytes 15343616 | tf_op jit(solution)/shard_map/qngd,knd->ngqk/dot_general | solution.py:125
  77.2 2.8 %fusion.3 = f32[4,512]{1,0:T(4,128)S(1)} fusion(f32[1536,512,4]{1,0,2:T(8,128)S(1)} %get-tuple-element.21, f32[4,512]{1,0:T(4,128)S(1)} %get-tuple-element.20, pred[512,1536]{0,1:T(8,128)(4,1)S(1)} %fusion.14), kind=kLoop, calls=%fused_computation.8 | loop fusion | flops 12580864 | bytes 13385728 | tf_op jit(solution)/shard_map/reduce_sum | solution.py:59
  79.9 0.0 copy-start.5
  79.9 0.0 copy-start.2
  80.0 3.9 %fusion.33 = bf16[128,4,512]{2,0,1:T(8,128)(2,1)S(1)} fusion(f32[4,512]{1,0:T(4,128)S(1)} %fusion.3, f32[4,512]{1,0:T(4,128)S(1)} %get-tuple-element.20, f32[1536,512,4]{1,0,2:T(8,128)S(1)} %get-tuple-element.21, pred[512,1536]{0,1:T(8,128)(4,1)S(1)} %fusion.14, bf16[1536,128]{1,0:T(8,128)(2,1)S(1)} %convolution_convert_fusion), kind=kOutput, calls=%fused_computation.55 | convolution fusion | flops 821297152 | bytes 14303232 | tf_op jit(solution)/shard_map/ngqk,knd->qngd/dot_general | solution.py:134
  83.9 0.0 copy-done.5
  83.9 0.5 fusion.21
  84.4 0.0 copy-done.2
  84.4 0.7 fusion.71
  85.1 1.3 convolution_add_fusion
  86.4 0.0 all-reduce.2.cloned.1.call-update
  86.4 0.0 all-gather.2.cloned.1.call-start
  86.5 37.5 %all-reduce.2.cloned.1.call-done = f32[8,4096]{1,0:T(8,128)} async-done(((f32[8,4096]{1,0:T(8,128)}), f32[8,4096]{1,0:T(8,128)}) %all-reduce.2.cloned.1.call-update) | async-done | bytes 131088 | tf_op jit(solution)/shard_map/psum | solution.py:156
  124.0 0.0 copy-start.7
  124.0 0.0 copy-start.8
  124.0 0.0 copy-start.9
  124.0 6.6 %multiply_reduce_fusion.2 = (f32[8]{0:T(128)S(1)}, f32[8,4096]{1,0:T(8,128)S(1)}) fusion(f32[8]{0:T(128)S(1)} %get-tuple-element.18, f32[8,4096]{1,0:T(8,128)} %all-reduce.2.cloned.1.call-done, bf16[1536,4096]{1,0:T(8,128)(2,1)} %param.11, s32[8]{0:T(128)S(1)} %get-tuple-element.19, s32[8]{0:T(128)S(1)} %copy-done.5), kind=kOutput, calls=%fused_computation.93 | convolution fusion | flops 100831224 | bytes 12845184 | tf_op jit(solution)/shard_map/dot_general | solution.py:146
  130.5 0.7 broadcast_multiply_fusion.1
  131.3 0.0 all-gather.2.cloned.1.call-update
  131.3 0.0 copy-done.7
  131.3 0.0 copy-done.8
  131.3 0.1 dynamic-slice_compare_fusion
  131.4 0.0 copy-done.9
  131.4 23.1 %all-gather.2.cloned.1.call-done = f32[64,4096]{1,0:T(8,128)} async-done(((f32[8,4096]{1,0:T(8,128)}), f32[64,4096]{1,0:T(8,128)}) %all-gather.2.cloned.1.call-update) | async-done | bytes 1048592 | tf_op jit(solution)/shard_map/all_gather | solution.py:169
  154.5 1.8 %multiply_reduce_fusion.1 = (f32[32]{0:T(128)S(1)}, f32[32,4096]{1,0:T(8,128)S(1)}) fusion(f32[64,4096]{1,0:T(8,128)} %all-gather.2.cloned.1.call-done, s32[64]{0:T(128)S(1)} %multiply_add_fusion, pred[64]{0:T(512)(128)(4,1)S(1)} %broadcast_compare_fusion.3), kind=kOutput, calls=%fused_computation.75 | convolution fusion | flops 100929504 | bytes 1573312 | tf_op jit(solution)/shard_map/dot_general | solution.py:168
  156.3 0.1 broadcast_multiply_fusion
  156.5 1.4 multiply_reduce_fusion
  157.9 0.7 constant_dynamic-slice_fusion
  158.6 0.2 fusion.73
  158.8 0.2 exponential_reduce_fusion
  159.0 0.7 subtract_select_fusion
  159.6 0.0 copy-done.1
  (16 shorter events, 0.1 us)
Async XLA Ops:
  7.2 16.7 %copy-start = (bf16[4096,128]{1,0:T(8,128)(2,1)S(1)}, bf16[4096,128]{1,0:T(8,128)(2,1)}, u32[]{:S(2)}) copy-start(bf16[4096,128]{1,0:T(8,128)(2,1)} %param.15) | copy-start | bytes 3145732
  7.2 116.8 %all-reduce.2.cloned.1.call-start = ((), (), s32[]{:S(2)}) async-start(), calls=%async_computation | async-start | bytes 262144 | tf_op jit(solution)/shard_map/psum | solution.py:156
  8.8 7.1 %copy-start.3 = (s32[1536]{0:T(1024)}, s32[1536]{0:T(1024)S(1)}, u32[]{:S(2)}) copy-start(s32[1536]{0:T(1024)S(1)} %broadcast_add_fusion) | copy-start | bytes 18436
  8.8 7.1 %copy-start.6 = (bf16[4096]{0:T(1024)(128)(2,1)S(1)}, bf16[4096]{0:T(1024)(128)(2,1)}, u32[]{:S(2)}) copy-start(bf16[4096]{0:T(1024)(128)(2,1)} %param.12) | copy-start | bytes 24580
  51.7 5.9 %slice-start = ((s32[1536]{0:T(1024)}), s32[1024]{0:T(1024)S(1)}, s32[]{:S(2)}) async-start(s32[1536]{0:T(1024)} %copy-done.3), calls=%async_computation.2 | async-start | bytes 8192 | tf_op jit(solution)/shard_map/slice | solution.py:46
  69.9 2.7 %copy-start.4 = (s32[1536]{0:T(1024)S(1)}, s32[1536]{0:T(1024)}, u32[]{:S(2)}) copy-start(s32[1536]{0:T(1024)} %copy-done.3) | copy-start | bytes 18436
  79.9 4.0 %copy-start.5 = (s32[8]{0:T(128)S(1)}, s32[8]{0:T(128)}, u32[]{:S(2)}) copy-start(s32[8]{0:T(128)} %param.17) | copy-start | bytes 100
  79.9 4.5 %copy-start.2 = (bf16[512,4096]{1,0:T(8,128)(2,1)S(1)}, bf16[512,4096]{1,0:T(8,128)(2,1)}, u32[]{:S(2)}) copy-start(bf16[512,4096]{1,0:T(8,128)(2,1)} %param.16) | copy-start | bytes 12582916
  86.4 68.1 %all-gather.2.cloned.1.call-start = ((), (), s32[]{:S(2)}) async-start(), calls=%async_computation.1 | async-start | bytes 1179648 | tf_op jit(solution)/shard_map/all_gather | solution.py:169
  124.0 7.4 %copy-start.7 = (s32[64]{0:T(128)S(1)}, s32[64]{0:T(128)}, u32[]{:S(2)}) copy-start(s32[64]{0:T(128)} %param.21) | copy-start | bytes 772
  124.0 7.4 %copy-start.8 = (s32[64]{0:T(128)S(1)}, s32[64]{0:T(128)}, u32[]{:S(2)}) copy-start(s32[64]{0:T(128)} %param.19) | copy-start | bytes 772
  124.0 7.5 %copy-start.9 = (s32[64]{0:T(128)S(1)}, s32[64]{0:T(128)}, u32[]{:S(2)}) copy-start(s32[64]{0:T(128)} %param.20) | copy-start | bytes 772
  124.0 35.7 %copy-start.1 = (bf16[4096,128]{1,0:T(8,128)(2,1)S(1)}, bf16[4096,128]{1,0:T(8,128)(2,1)}, u32[]{:S(2)}) copy-start(bf16[4096,128]{1,0:T(8,128)(2,1)} %param.15) | copy-start | bytes 3145732
Sparse Core Ops, SparseCore 0:
  86.6 37.3 all-reduce.1
  131.4 23.0 all-gather.1
where the time goes:
time: 167 us; the launch traced here: 166 us
  waiting for transfers between devices  60.6 us (36%)
  matrix products  43.6 us (26%)
  other arithmetic  38.3 us (23%)
  between operations  14.4 us (9%)
  local copies, waits for them, and re-layouts  9.62 us (6%)
    psum x1, waiting for transfers between devices, per_device(): pooled = (token_sums + lax.psum(head_part, 'mp')) / token_counts  37.5 us
    all_gather x1, waiting for transfers between devices, per_device(): lax.all_gather(embedded, 'dp', axis=0, tiled=True)  23.1 us
    dot_general x1, matrix products, per_device(): jnp.dot(normed, w_query, preferred_element_type=jnp.float32)  9.66 us
    dot_general x3, matrix products, per_device(): jnp.einsum('ngqk,knd->qngd', attention_probs, values_all[:key_end], prefe...  8.09 us
    convert_element_type x1, other arithmetic, per_device(): normed = (widened * lax.rsqrt(jnp.mean(widened * widened, axis=-1, keepdi...  7.88 us
    reduce_sum x1, other arithmetic, per_device(): jnp.mean(widened * widened, axis=-1, keepdims=True) + 1e-05  7.07 us
    dot_general x1, matrix products, per_device(): token_sums = jnp.dot(member, tokens, preferred_element_type=jnp.float32)  6.55 us
    dot_general x3, matrix products, per_device(): jnp.einsum('qngd,knd->ngqk', block_queries, keys_rot[:key_end], preferred...  5.99 us
  transfers between devices with their start and end apart: 2, of which 2 were waited for; matrix products, arithmetic and copies ran while one was open for 0% of the time, Pallas kernels for 0%

commit v1 on v0

v1 whole, which is shorter than its diff:
```python
import functools
import math

import numpy as np
import jax
import jax.numpy as jnp
from jax import lax
from jax.experimental import pallas as pl
from jax.experimental.pallas import tpu as pltpu
from jax.sharding import PartitionSpec as P

HEAD_DIM = 128
WAYS = 32
ROPE_BASE = 500000.0
NEG_FILL = -1e30
MESH = pl.DeviceIdType.MESH
F32 = jnp.float32
BF16 = jnp.bfloat16
HIGHEST = lax.Precision.HIGHEST


def pick(total, options):
    for candidate in options:
        if total % candidate == 0:
            return candidate
    return total


def encode_kernel(
    dims, st_ref, ln_ref, x_ref, gain_ref, wq_hbm, wk_hbm, wv_hbm, wo_hbm, cos_ref, sin_ref,
    hp_ref, ts_ref, w_s, wo_s, q_s, k_s, v_s, s_s, c_s, w_sem, wo_sem,
):
    rows, tile, qb, width, slots, heads, chunk, share, n_mp = dims
    hd = HEAD_DIM
    i = pl.program_id(0)
    last = pl.num_programs(0) - 1
    q_cols = heads * hd
    chunks = width // chunk
    rank = lax.axis_index("mp")
    wo_copy = pltpu.make_async_copy(wo_hbm, wo_s, wo_sem)

    def members(first, count):
        slot = lax.broadcasted_iota(jnp.int32, (slots, count), 0)
        token = lax.broadcasted_iota(jnp.int32, (slots, count), 1) + first
        lo = jnp.zeros((slots, count), jnp.int32)
        hi = jnp.zeros((slots, count), jnp.int32)
        for j in range(slots):
            lo = jnp.where(slot == j, st_ref[j], lo)
            hi = jnp.where(slot == j, st_ref[j] + ln_ref[j], hi)
        return jnp.where((token >= lo) & (token < hi), 1.0, 0.0).astype(BF16)

    @pl.when(i == 0)
    def _():
        def copies(c):
            r = pl.ds(c * chunk, chunk)
            return (
                pltpu.make_async_copy(wq_hbm.at[r, :], w_s.at[r, pl.ds(0, q_cols)], w_sem.at[c, 0]),
                pltpu.make_async_copy(wk_hbm.at[r, :], w_s.at[r, pl.ds(q_cols, hd)], w_sem.at[c, 1]),
                pltpu.make_async_copy(wv_hbm.at[r, :], w_s.at[r, pl.ds(q_cols + hd, hd)], w_sem.at[c, 2]),
            )

        for c in range(chunks):
            for copy in copies(c):
                copy.start()
        wo_copy.start()
        ts_ref[...] = jnp.zeros_like(ts_ref)
        c_s[...] = jnp.zeros_like(c_s)
        for c in range(chunks):
            for copy in copies(c):
                copy.wait()
            for b in range(chunk // 128):
                at = c * chunk + b * 128
                g = jnp.broadcast_to(gain_ref[:, at : at + 128].astype(F32), (128, 128)).T
                for v in range(heads + 2):
                    w = w_s[at : at + 128, v * hd : (v + 1) * hd].astype(F32)
                    w_s[at : at + 128, v * hd : (v + 1) * hd] = (w * g).astype(BF16)

    half = tile // 2
    sums = []
    for b in range(2):
        acc = jnp.zeros((half, 128), F32)
        for v in range(width // 128):
            x = x_ref[b * half : (b + 1) * half, v * 128 : (v + 1) * 128].astype(F32)
            acc = acc + x * x
        sums.append(jnp.sum(acc, axis=-1, keepdims=True))
    rstd = lax.rsqrt(jnp.concatenate(sums, axis=0) / width + 1e-05)
    proj = jnp.dot(x_ref[...], w_s[...], preferred_element_type=F32)
    cos = cos_ref[...]
    sin = sin_ref[...]

    def rope(y):
        return (y * cos + pltpu.roll(y, hd // 2, 1) * sin).astype(BF16)

    q_rstd = rstd * (math.log2(math.e) / math.sqrt(hd))
    for h in range(heads):
        q_s[h] = rope(proj[:, h * hd : (h + 1) * hd] * q_rstd)
    here = pl.ds(pl.multiple_of(i * tile, tile), tile)
    k_s[here, :] = rope(proj[:, q_cols : q_cols + hd] * rstd)
    v_s[here, :] = (proj[:, q_cols + hd :] * rstd).astype(BF16)
    cols = pl.ds(pl.multiple_of(rank * share, share), share)
    ts_ref[...] += jnp.dot(members(i * tile, tile), x_ref[:, cols], preferred_element_type=F32)

    for b in range(tile // qb):
        block = i * (tile // qb) + b
        first = block * qb
        lo_row = first
        token = lax.broadcasted_iota(jnp.int32, (1, qb), 1) + first
        start = token
        for j in range(slots):
            s0 = st_ref[j]
            s1 = s0 + ln_ref[j]
            start = jnp.where((token >= s0) & (token < s1), s0, start)
            lo_row = jnp.where((first >= s0) & (first < s1), s0, lo_row)
        lo = lo_row // qb

        def fold(a, op):
            return op(a.reshape(qb // 8, 8, qb), axis=0)

        def score(kb, peaks):
            at = pl.ds(pl.multiple_of(kb * qb, qb), qb)
            keys = k_s[at, :]
            row = lax.broadcasted_iota(jnp.int32, (qb, qb), 0) + kb * qb
            ok = (row >= start) & (row <= token)
            out = []
            for h in range(heads):
                s = lax.dot_general(
                    keys, q_s[h, b * qb : (b + 1) * qb, :], (((1,), (1,)), ((), ())),
                    preferred_element_type=F32,
                )
                s = jnp.where(ok, s, NEG_FILL)
                s_s[at, h * qb : (h + 1) * qb] = s
                out.append(jnp.maximum(peaks[h], fold(s, jnp.max)))
            return tuple(out)

        peaks = lax.fori_loop(
            lo, block + 1, score, tuple(jnp.full((8, qb), NEG_FILL, F32) for _ in range(heads))
        )
        peaks = [jnp.max(p, axis=0, keepdims=True) for p in peaks]

        def expo(kb, totals):
            at = pl.ds(pl.multiple_of(kb * qb, qb), qb)
            out = []
            for h in range(heads):
                e = jnp.exp2(s_s[at, h * qb : (h + 1) * qb] - peaks[h])
                s_s[at, h * qb : (h + 1) * qb] = e
                out.append(totals[h] + fold(e, jnp.sum))
            return tuple(out)

        totals = lax.fori_loop(
            lo, block + 1, expo, tuple(jnp.zeros((8, qb), F32) for _ in range(heads))
        )
        inverse = [1.0 / jnp.sum(t, axis=0, keepdims=True) for t in totals]

        def gather(kb, carry):
            at = pl.ds(pl.multiple_of(kb * qb, qb), qb)
            for h in range(heads):
                part = c_s[h, at, :]
                for v in range(qb // 128):
                    e = s_s[at, h * qb + v * 128 : h * qb + (v + 1) * 128]
                    part = part + e * inverse[h][:, v * 128 : (v + 1) * 128]
                c_s[h, at, :] = part
            return carry

        lax.fori_loop(lo, block + 1, gather, 0)

    @pl.when(i == last)
    def _():
        member = members(0, rows)
        parts = []
        for h in range(heads):
            mass = jnp.sum(c_s[h], axis=-1, keepdims=True)
            mixed = mass * v_s[...].astype(F32)
            high = mixed.astype(BF16)
            low = (mixed - high.astype(F32)).astype(BF16)
            parts.append(
                jnp.dot(member, high, preferred_element_type=F32)
                + jnp.dot(member, low, preferred_element_type=F32)
            )
        attended = jnp.concatenate(parts, axis=-1)
        high = attended.astype(BF16)
        low = (attended - high.astype(F32)).astype(BF16)
        wo_copy.wait()
        for p in range(n_mp):
            w = wo_s[:, p * share : (p + 1) * share]
            hp_ref[p] = jnp.dot(high, w, preferred_element_type=F32) + jnp.dot(
                low, w, preferred_element_type=F32
            )


def score_kernel(
    dims, hp_ref, ts_ref, ln_ref, ep_ref, cl_ref, fl_ref, lp_ref, pr_ref,
    rs_buf, ag_buf, g_buf, d_buf, rs_send, rs_recv, ag_send, ag_recv, g_send, g_recv,
):
    n_dp, n_mp, slots, share, width, nseq, classes = dims
    dp = lax.axis_index("dp")
    mp = lax.axis_index("mp")
    barrier = pltpu.get_barrier_semaphore()
    for d in range(1, n_mp):
        pl.semaphore_signal(barrier, inc=1, device_id=(dp, lax.rem(mp + d, n_mp)), device_id_type=MESH)
    for d in range(1, n_dp):
        pl.semaphore_signal(barrier, inc=1, device_id=(lax.rem(dp + d, n_dp), mp), device_id_type=MESH)
    pl.semaphore_wait(barrier, n_mp + n_dp - 2)

    rs = []
    for d in range(1, n_mp):
        peer = lax.rem(mp + d, n_mp)
        rs.append(pltpu.make_async_remote_copy(
            src_ref=hp_ref.at[peer], dst_ref=rs_buf.at[d - 1], send_sem=rs_send.at[d - 1],
            recv_sem=rs_recv.at[d - 1], device_id=(dp, peer), device_id_type=MESH,
        ))
        rs[-1].start()
    pooled = ts_ref[...] + hp_ref[mp]
    slot = lax.broadcasted_iota(jnp.int32, (slots, share), 0)
    count = jnp.ones((slots, share), F32)
    for j in range(slots):
        count = jnp.where(slot == j, ln_ref[j].astype(F32), count)
    for d in range(1, n_mp):
        rs[d - 1].wait_recv()
        pooled = pooled + rs_buf[d - 1]
    own = pl.ds(pl.multiple_of(dp * slots, slots), slots)
    ag_buf[own, :] = pooled / count

    ag = []
    for d in range(1, n_dp):
        peer = lax.rem(dp + d, n_dp)
        ag.append(pltpu.make_async_remote_copy(
            src_ref=ag_buf.at[own, :], dst_ref=ag_buf.at[own, :], send_sem=ag_send.at[d - 1],
            recv_sem=ag_recv.at[d - 1], device_id=(peer, mp), device_id_type=MESH,
        ))
        ag[-1].start()
    for d in range(1, n_mp):
        rs[d - 1].wait_send()
    for d in range(1, n_dp):
        ag[d - 1].wait_recv()

    every = ag_buf[...]
    g_buf[mp] = lax.dot_general(
        every, every, (((1,), (1,)), ((), ())), precision=HIGHEST, preferred_element_type=F32
    )
    gs = []
    for d in range(1, n_mp):
        peer = lax.rem(mp + d, n_mp)
        gs.append(pltpu.make_async_remote_copy(
            src_ref=g_buf.at[mp], dst_ref=g_buf.at[mp], send_sem=g_send.at[d - 1],
            recv_sem=g_recv.at[d - 1], device_id=(dp, peer), device_id_type=MESH,
        ))
        gs[-1].start()
    for d in range(1, n_dp):
        ag[d - 1].wait_send()

    label = ep_ref[...] * WAYS + cl_ref[...]
    support = fl_ref[...] == 0
    class_row = lax.broadcasted_iota(jnp.int32, (classes, nseq), 0)
    select = jnp.where((class_row == label) & support, 1.0, 0.0)
    a = lax.broadcasted_iota(jnp.int32, (slots, nseq), 0) + dp * slots
    mine = a == lax.broadcasted_iota(jnp.int32, (slots, nseq), 1)
    own_query = jnp.sum(jnp.where(mine, fl_ref[...].astype(F32), 0.0), axis=-1, keepdims=True)
    own_episode = jnp.sum(jnp.where(mine, ep_ref[...].astype(F32), 0.0), axis=-1, keepdims=True)

    for d in range(1, n_mp):
        gs[d - 1].wait_recv()
    gram = g_buf[0]
    for p in range(1, n_mp):
        gram = gram + g_buf[p]
    eye = lax.broadcasted_iota(jnp.int32, (nseq, nseq), 0) == lax.broadcasted_iota(
        jnp.int32, (nseq, nseq), 1
    )
    diag = jnp.where(eye, gram, 0.0)
    scale_row = lax.rsqrt(jnp.sum(diag, axis=0, keepdims=True) / width + 1e-06)
    scale_col = lax.rsqrt(jnp.sum(diag, axis=1, keepdims=True) / width + 1e-06)
    gram = gram * scale_row * scale_col
    cross_t = jnp.dot(select, gram, precision=HIGHEST, preferred_element_type=F32)
    norm_col = jnp.maximum(jnp.sum(cross_t * select, axis=1, keepdims=True), 0.0)
    proto_col = lax.rsqrt(norm_col / width + 1e-06)
    sums = jnp.dot(select * scale_row, every, precision=HIGHEST, preferred_element_type=F32)
    pr_ref[...] = sums * proto_col

    d_buf[...] = gram
    mine_gram = d_buf[own, :]
    cross = lax.dot_general(
        mine_gram, select, (((1,), (1,)), ((), ())), precision=HIGHEST, preferred_element_type=F32
    )
    eye_c = lax.broadcasted_iota(jnp.int32, (classes, classes), 0) == lax.broadcasted_iota(
        jnp.int32, (classes, classes), 1
    )
    norm_row = jnp.sum(jnp.where(eye_c, norm_col, 0.0), axis=0, keepdims=True)
    proto_row = lax.rsqrt(norm_row / width + 1e-06)
    own_norm = jnp.sum(jnp.where(mine, mine_gram, 0.0), axis=-1, keepdims=True)
    distance = own_norm - 2.0 * (cross * proto_row) + norm_row * proto_row * proto_row
    picked = jnp.zeros((slots, WAYS), F32)
    for e in range(classes // WAYS):
        picked = jnp.where(own_episode == float(e), distance[:, e * WAYS : (e + 1) * WAYS], picked)
    logits = -picked / math.sqrt(width)
    shifted = logits - jnp.max(logits, axis=-1, keepdims=True)
    logp = shifted - jnp.log(jnp.sum(jnp.exp(shifted), axis=-1, keepdims=True))
    lp_ref[...] = jnp.where(own_query == 1.0, logp, 0.0)
    for d in range(1, n_mp):
        gs[d - 1].wait_send()


def per_device(
    n_dp, n_mp, tokens, norm_gain, w_query, w_key, w_value, w_out,
    seq_starts, seq_lengths, episode_ids, class_ids, query_flags,
):
    rows, width = tokens.shape
    slots = seq_starts.shape[0]
    hd = HEAD_DIM
    heads = w_query.shape[1] // hd
    assert w_key.shape[1] == hd
    share = width // n_mp
    tile = pick(rows, (512, 256, 128))
    qb = pick(tile, (256, 128))
    chunk = pick(width, (512, 256, 128))
    frequency = ROPE_BASE ** (-np.arange(hd // 2, dtype=np.float64) * 2.0 / hd)
    angles = np.arange(rows, dtype=np.float64)[:, None] * frequency[None, :]
    cos = jnp.asarray(np.concatenate([np.cos(angles)] * 2, axis=1), F32)
    sin = jnp.asarray(np.concatenate([-np.sin(angles), np.sin(angles)], axis=1), F32)
    smem = pl.BlockSpec(memory_space=pltpu.SMEM)
    vmem = pl.BlockSpec(memory_space=pltpu.VMEM)
    hbm = pl.BlockSpec(memory_space=pl.ANY)
    dims = (rows, tile, qb, width, slots, heads, chunk, share, n_mp)
    head_part, token_sums = pl.pallas_call(
        functools.partial(encode_kernel, dims),
        grid=(rows // tile,),
        out_shape=(
            jax.ShapeDtypeStruct((n_mp, slots, share), F32),
            jax.ShapeDtypeStruct((slots, share), F32),
        ),
        in_specs=[
            smem, smem,
            pl.BlockSpec((tile, width), lambda i: (i, 0)),
            pl.BlockSpec((1, width), lambda i: (0, 0)),
            hbm, hbm, hbm, hbm,
            pl.BlockSpec((tile, hd), lambda i: (i, 0)),
            pl.BlockSpec((tile, hd), lambda i: (i, 0)),
        ],
        out_specs=(
            pl.BlockSpec((n_mp, slots, share), lambda i: (0, 0, 0)),
            pl.BlockSpec((slots, share), lambda i: (0, 0)),
        ),
        scratch_shapes=[
            pltpu.VMEM((width, (heads + 2) * hd), BF16),
            pltpu.VMEM(w_out.shape, BF16),
            pltpu.VMEM((heads, tile, hd), BF16),
            pltpu.VMEM((rows, hd), BF16),
            pltpu.VMEM((rows, hd), BF16),
            pltpu.VMEM((rows, heads * qb), F32),
            pltpu.VMEM((heads, rows, hd), F32),
            pltpu.SemaphoreType.DMA((width // chunk, 3)),
            pltpu.SemaphoreType.DMA,
        ],
        compiler_params=pltpu.CompilerParams(
            dimension_semantics=("arbitrary",), vmem_limit_bytes=60 * 1024 * 1024
        ),
    )(
        seq_starts, seq_lengths, tokens, norm_gain.reshape(1, width),
        w_query, w_key, w_value, w_out, cos, sin,
    )
    nseq = episode_ids.shape[0]
    episodes = max(1, nseq // (2 * WAYS))
    classes = episodes * WAYS
    dims = (n_dp, n_mp, slots, share, width, nseq, classes)
    dma = pltpu.SemaphoreType.DMA
    return pl.pallas_call(
        functools.partial(score_kernel, dims),
        out_shape=(
            jax.ShapeDtypeStruct((slots, WAYS), F32),
            jax.ShapeDtypeStruct((classes, share), F32),
        ),
        in_specs=[vmem, vmem, smem, vmem, vmem, vmem],
        out_specs=(vmem, vmem),
        scratch_shapes=[
            pltpu.VMEM((n_mp - 1, slots, share), F32),
            pltpu.VMEM((nseq, share), F32),
            pltpu.VMEM((n_mp, nseq, nseq), F32),
            pltpu.VMEM((nseq, nseq), F32),
            dma((n_mp - 1,)), dma((n_mp - 1,)),
            dma((n_dp - 1,)), dma((n_dp - 1,)),
            dma((n_mp - 1,)), dma((n_mp - 1,)),
        ],
        compiler_params=pltpu.CompilerParams(collective_id=0, has_side_effects=True),
    )(
        head_part, token_sums, seq_lengths,
        episode_ids.reshape(1, nseq), class_ids.reshape(1, nseq), query_flags.reshape(1, nseq),
    )


def solution(mesh):
    placed = (
        P("dp", None), P(), P(None, "mp"), P(None, "mp"), P(None, "mp"), P("mp", None),
        P("dp"), P("dp"), P(), P(), P(),
    )
    return jax.shard_map(
        functools.partial(per_device, mesh.shape["dp"], mesh.shape["mp"]),
        mesh=mesh,
        in_specs=placed,
        out_specs=(P("dp", None), P(None, "mp")),
        check_vma=False,
    )
```

time: 167 us -> 54 us (0.32)
  waiting for transfers between devices: 60.6 us -> 0 us
  Pallas kernels: 0 us -> 49.1 us
  matrix products: 43.6 us -> 0 us
  other arithmetic: 38.3 us -> 0 us
  between operations: 14.4 us -> 0.65 us
  local copies, waits for them, and re-layouts: 9.62 us -> 4.14 us
    pallas_call x0 -> x2, Pallas kernels: none -> 49.1 us  [the longest x1 26.9 us: per_device(): pl.pallas_call(functools.partial(encode_kernel, dims), grid=(rows // tile...]
    dot_general x14 -> x0, matrix products: 43.6 us -> none  [the longest x1 9.66 us: per_device(): jnp.dot(normed, w_query, preferred_element_type=jnp.float32)]
    psum x1 -> x0, waiting for transfers between devices: 37.5 us -> none  [per_device(): pooled = (token_sums + lax.psum(head_part, 'mp')) / token_counts]
    all_gather x1 -> x0, waiting for transfers between devices: 23.1 us -> none  [per_device(): lax.all_gather(embedded, 'dp', axis=0, tiled=True)]
    reduce_sum x7 -> x0, other arithmetic: 15 us -> none  [the longest x1 7.07 us: per_device(): jnp.mean(widened * widened, axis=-1, keepdims=True) + 1e-05]
    convert_element_type x4 -> x0, other arithmetic: 8.65 us -> none  [the longest x1 7.88 us: per_device(): normed = (widened * lax.rsqrt(jnp.mean(widened * widened, axis=-1, keepdi...]
    another operation x2 -> x0, other arithmetic: 5.66 us -> none
    cos x1 -> x0, other arithmetic: 4.3 us -> none  [rotate(): cosine = jnp.cos(angles)[:, None, :]]
  transfers between devices with their start and end apart: 2 -> 0, of which waited for: 2 -> 0; matrix products, arithmetic and copies ran while one was open for 0% -> 0% of each run, Pallas kernels for 0% -> 0%
where the time goes in v1:
time: 54 us; the launch traced here: 53.9 us
  Pallas kernels  49.1 us (91%)
  local copies, waits for them, and re-layouts  4.14 us (8%)
  between operations  0.65 us (1%)
    pallas_call x1, Pallas kernels, per_device(): pl.pallas_call(functools.partial(encode_kernel, dims), grid=(rows // tile...  26.9 us
    pallas_call x1, Pallas kernels, per_device(): pl.pallas_call(functools.partial(score_kernel, dims), out_shape=(jax.Shap...  22.2 us
    unnamed x2, local copies, waits for them, and re-layouts  2.83 us
    reshape x1, local copies, waits for them, and re-layouts, per_device(): norm_gain.reshape(1, width)  1.31 us

profile of v1, /device:TPU:0, one launch (start us, length us, event | category | flops | bytes accessed | tf_op | source)
XLA Modules:
  0.0 53.9 jit_solution(5568451901975739633)
XLA Ops:
  0.6 1.3 %reshape.16.gain_ref = bf16[1,4096]{1,0:T(2,128)(2,1)} reshape(bf16[4096]{0:T(1024)(128)(2,1)} %param.14) | data formatting | bytes 16384 | tf_op jit(solution)/shard_map/reshape | solution.py:356
  1.9 26.9 %shard_map.140 = (f32[4,8,1024]{2,1,0:T(8,128)}, f32[8,1024]{1,0:T(8,128)}) custom-call(s32[8]{0:T(128)} %st_ref.1, s32[8]{0:T(128)} %ln_ref.3, bf16[1536,4096]{1,0:T(8,128)(2,1)} %x_ref.1, bf16[1,4096]{1,0:T(2,128)(2,1)} %reshape.16.gain_ref, bf16[4096,512]{1,0:T(8,128)(2,1)} %wq_hbm.1, bf16[4096,128]{1,0:T(8,128)(2,1)} %wk_hbm.1, ...), custom_call_target="tpu_custom_call" | custom-call | tf_op jit(solution)/shard_map/pallas_call | solution.py:322
  28.8 22.2 %shard_map.141 = (f32[8,32]{1,0:T(8,128)}, f32[32,1024]{1,0:T(8,128)}) custom-call(f32[4,8,1024]{2,1,0:T(8,128)} %get-tuple-element.4.hp_ref, f32[8,1024]{1,0:T(8,128)} %get-tuple-element.5.ts_ref, s32[8]{0:T(128)} %ln_ref.3, s32[1,64]{1,0:T(1,128)} %bitcast.3, s32[1,64]{1,0:T(1,128)} %bitcast.4, s32[1,64]{1,0:T(1,128)} %bitcast.5), custom_call_target="tpu_custom_call" | custom-call | tf_op jit(solution)/shard_map/pallas_call | solution.py:364
  51.0 1.3 %copy.17 = f32[8,32]{1,0:T(8,128)} copy(f32[8,32]{1,0:T(8,128)} %get-tuple-element.8) | data formatting | bytes 2048
  52.3 1.6 %copy.18 = f32[32,1024]{1,0:T(8,128)} copy(f32[32,1024]{1,0:T(8,128)} %get-tuple-element.9) | data formatting | bytes 262144

commit v2 on v1

--- a/solution.py
+++ b/solution.py
@@ -27,8 +27,8 @@
 
 
 def encode_kernel(
-    dims, st_ref, ln_ref, x_ref, gain_ref, wq_hbm, wk_hbm, wv_hbm, wo_hbm, cos_ref, sin_ref,
-    hp_ref, ts_ref, w_s, wo_s, q_s, k_s, v_s, s_s, c_s, w_sem, wo_sem,
+    dims, st_ref, ln_ref, x_hbm, gain_ref, wq_hbm, wk_hbm, wv_hbm, wo_hbm, cos_ref, sin_ref,
+    hp_ref, ts_ref, x_s, acc_s, sq_s, w_s, wo_s, q_s, k_s, v_s, s_s, c_s, w_sem, wo_sem, x0_sem, x_sem,
 ):
     rows, tile, qb, width, slots, heads, chunk, share, n_mp = dims
     hd = HEAD_DIM
@@ -38,6 +38,22 @@
     chunks = width // chunk
     rank = lax.axis_index("mp")
     wo_copy = pltpu.make_async_copy(wo_hbm, wo_s, wo_sem)
+    now = lax.rem(i, 2)
+    x_ref = x_s.at[now]
+
+    def fetch(t, slot):
+        r = pl.ds(pl.multiple_of(t * tile, tile), tile)
+        return pltpu.make_async_copy(x_hbm.at[r, :], x_s.at[slot], x_sem.at[slot])
+
+    def squares(at, count, add):
+        half = tile // 2
+        for b in range(2):
+            r = slice(b * half, (b + 1) * half)
+            acc = sq_s[r, :] if add else jnp.zeros((half, 128), F32)
+            for v in range(at, at + count, 128):
+                x = x_ref[r, v : v + 128].astype(F32)
+                acc = acc + x * x
+            sq_s[r, :] = acc
 
     def members(first, count):
         slot = lax.broadcasted_iota(jnp.int32, (slots, count), 0)
@@ -54,6 +70,7 @@
         def copies(c):
             r = pl.ds(c * chunk, chunk)
             return (
+                pltpu.make_async_copy(x_hbm.at[pl.ds(0, tile), r], x_s.at[0, :, r], x0_sem.at[c]),
                 pltpu.make_async_copy(wq_hbm.at[r, :], w_s.at[r, pl.ds(0, q_cols)], w_sem.at[c, 0]),
                 pltpu.make_async_copy(wk_hbm.at[r, :], w_s.at[r, pl.ds(q_cols, hd)], w_sem.at[c, 1]),
                 pltpu.make_async_copy(wv_hbm.at[r, :], w_s.at[r, pl.ds(q_cols + hd, hd)], w_sem.at[c, 2]),
@@ -62,6 +79,8 @@
         for c in range(chunks):
             for copy in copies(c):
                 copy.start()
+        if rows > tile:
+            fetch(1, 1).start()
         wo_copy.start()
         ts_ref[...] = jnp.zeros_like(ts_ref)
         c_s[...] = jnp.zeros_like(c_s)
@@ -70,21 +89,28 @@
                 copy.wait()
             for b in range(chunk // 128):
                 at = c * chunk + b * 128
-                g = jnp.broadcast_to(gain_ref[:, at : at + 128].astype(F32), (128, 128)).T
+                g = jnp.broadcast_to(gain_ref[at : at + 128].astype(F32)[None, :], (128, 128)).T
                 for v in range(heads + 2):
                     w = w_s[at : at + 128, v * hd : (v + 1) * hd].astype(F32)
                     w_s[at : at + 128, v * hd : (v + 1) * hd] = (w * g).astype(BF16)
-
-    half = tile // 2
-    sums = []
-    for b in range(2):
-        acc = jnp.zeros((half, 128), F32)
-        for v in range(width // 128):
-            x = x_ref[b * half : (b + 1) * half, v * 128 : (v + 1) * 128].astype(F32)
-            acc = acc + x * x
-        sums.append(jnp.sum(acc, axis=-1, keepdims=True))
-    rstd = lax.rsqrt(jnp.concatenate(sums, axis=0) / width + 1e-05)
-    proj = jnp.dot(x_ref[...], w_s[...], preferred_element_type=F32)
+            r = slice(c * chunk, (c + 1) * chunk)
+            part = jnp.dot(x_s[0, :, r], w_s[r, :], preferred_element_type=F32)
+            acc_s[...] = part if c == 0 else acc_s[...] + part
+            squares(c * chunk, chunk, c > 0)
+
+    @pl.when(i > 0)
+    def _():
+        fetch(i, now).wait()
+
+        @pl.when(i < last)
+        def _():
+            fetch(i + 1, 1 - now).start()
+
+        acc_s[...] = jnp.dot(x_ref[...], w_s[...], preferred_element_type=F32)
+        squares(0, width, False)
+
+    rstd = lax.rsqrt(jnp.sum(sq_s[...], axis=-1, keepdims=True) / width + 1e-05)
+    proj = acc_s
     cos = cos_ref[...]
     sin = sin_ref[...]
 
@@ -96,7 +122,7 @@
         q_s[h] = rope(proj[:, h * hd : (h + 1) * hd] * q_rstd)
     here = pl.ds(pl.multiple_of(i * tile, tile), tile)
     k_s[here, :] = rope(proj[:, q_cols : q_cols + hd] * rstd)
-    v_s[here, :] = (proj[:, q_cols + hd :] * rstd).astype(BF16)
+    v_s[here, :] = (proj[:, q_cols + hd : q_cols + 2 * hd] * rstd).astype(BF16)
     cols = pl.ds(pl.multiple_of(rank * share, share), share)
     ts_ref[...] += jnp.dot(members(i * tile, tile), x_ref[:, cols], preferred_element_type=F32)
 
@@ -170,28 +196,23 @@
         for h in range(heads):
             mass = jnp.sum(c_s[h], axis=-1, keepdims=True)
             mixed = mass * v_s[...].astype(F32)
-            high = mixed.astype(BF16)
-            low = (mixed - high.astype(F32)).astype(BF16)
-            parts.append(
-                jnp.dot(member, high, preferred_element_type=F32)
-                + jnp.dot(member, low, preferred_element_type=F32)
-            )
+            parts.append(jnp.dot(member, mixed.astype(BF16), preferred_element_type=F32))
         attended = jnp.concatenate(parts, axis=-1)
         high = attended.astype(BF16)
-        low = (attended - high.astype(F32)).astype(BF16)
+        low = attended - high.astype(F32)
+        both = jnp.concatenate([high.astype(F32), low], axis=0).astype(BF16)
         wo_copy.wait()
         for p in range(n_mp):
             w = wo_s[:, p * share : (p + 1) * share]
-            hp_ref[p] = jnp.dot(high, w, preferred_element_type=F32) + jnp.dot(
-                low, w, preferred_element_type=F32
-            )
-
-
-def score_kernel(
-    dims, hp_ref, ts_ref, ln_ref, ep_ref, cl_ref, fl_ref, lp_ref, pr_ref,
-    rs_buf, ag_buf, g_buf, d_buf, rs_send, rs_recv, ag_send, ag_recv, g_send, g_recv,
+            out = jnp.dot(both, w, preferred_element_type=F32)
+            hp_ref[p] = out[:slots] + out[slots:]
+
+
+def exchange_kernel(
+    dims, hp_ref, ts_ref, ln_ref, every_ref, gram_ref,
+    rs_buf, ag_buf, g_buf, rs_send, rs_recv, ag_send, ag_recv, g_send, g_recv,
 ):
-    n_dp, n_mp, slots, share, width, nseq, classes = dims
+    n_dp, n_mp, slots, share, nseq, pieces, fold = dims
     dp = lax.axis_index("dp")
     mp = lax.axis_index("mp")
     barrier = pltpu.get_barrier_semaphore()
@@ -201,53 +222,79 @@
         pl.semaphore_signal(barrier, inc=1, device_id=(lax.rem(dp + d, n_dp), mp), device_id_type=MESH)
     pl.semaphore_wait(barrier, n_mp + n_dp - 2)
 
-    rs = []
+    piece = share // pieces
+    rs = {}
+    for c in range(pieces):
+        cols = pl.ds(c * piece, piece)
+        for d in range(1, n_mp):
+            peer = lax.rem(mp + d, n_mp)
+            rs[c, d] = pltpu.make_async_remote_copy(
+                src_ref=hp_ref.at[peer, :, cols], dst_ref=rs_buf.at[d - 1, c],
+                send_sem=rs_send.at[c, d - 1], recv_sem=rs_recv.at[c, d - 1],
+                device_id=(dp, peer), device_id_type=MESH,
+            )
+            rs[c, d].start()
+    slot = lax.broadcasted_iota(jnp.int32, (slots, piece), 0)
+    count = jnp.ones((slots, piece), F32)
+    for j in range(slots):
+        count = jnp.where(slot == j, ln_ref[j].astype(F32), count)
+    own = pl.ds(pl.multiple_of(dp * slots, slots), slots)
+    ag = {}
+    for c in range(pieces):
+        cols = slice(c * piece, (c + 1) * piece)
+        pooled = ts_ref[:, cols] + hp_ref[mp, :, cols]
+        for d in range(1, n_mp):
+            rs[c, d].wait_recv()
+            pooled = pooled + rs_buf[d - 1, c]
+        ag_buf[c, own, :] = pooled / count
+        for d in range(1, n_dp):
+            peer = lax.rem(dp + d, n_dp)
+            ag[c, d] = pltpu.make_async_remote_copy(
+                src_ref=ag_buf.at[c, own, :], dst_ref=ag_buf.at[c, own, :],
+                send_sem=ag_send.at[c, d - 1], recv_sem=ag_recv.at[c, d - 1],
+                device_id=(peer, mp), device_id_type=MESH,
+            )
+            ag[c, d].start()
+    part = None
+    for c in range(pieces):
+        for d in range(1, n_dp):
+            ag[c, d].wait_recv()
+        block = ag_buf[c]
+        every_ref[:, c * piece : (c + 1) * piece] = block
+        term = lax.dot_general(
+            block, block, (((1,), (1,)), ((), ())), precision=HIGHEST, preferred_element_type=F32
+        )
+        part = term if part is None else part + term
+    tall = nseq // fold
+    g_buf[mp] = jnp.concatenate([part[f * tall : (f + 1) * tall] for f in range(fold)], axis=1)
+    gs = {}
     for d in range(1, n_mp):
         peer = lax.rem(mp + d, n_mp)
-        rs.append(pltpu.make_async_remote_copy(
-            src_ref=hp_ref.at[peer], dst_ref=rs_buf.at[d - 1], send_sem=rs_send.at[d - 1],
-            recv_sem=rs_recv.at[d - 1], device_id=(dp, peer), device_id_type=MESH,
-        ))
-        rs[-1].start()
-    pooled = ts_ref[...] + hp_ref[mp]
-    slot = lax.broadcasted_iota(jnp.int32, (slots, share), 0)
-    count = jnp.ones((slots, share), F32)
-    for j in range(slots):
-        count = jnp.where(slot == j, ln_ref[j].astype(F32), count)
-    for d in range(1, n_mp):
-        rs[d - 1].wait_recv()
-        pooled = pooled + rs_buf[d - 1]
-    own = pl.ds(pl.multiple_of(dp * slots, slots), slots)
-    ag_buf[own, :] = pooled / count
-
-    ag = []
-    for d in range(1, n_dp):
-        peer = lax.rem(dp + d, n_dp)
-        ag.append(pltpu.make_async_remote_copy(
-            src_ref=ag_buf.at[own, :], dst_ref=ag_buf.at[own, :], send_sem=ag_send.at[d - 1],
-            recv_sem=ag_recv.at[d - 1], device_id=(peer, mp), device_id_type=MESH,
-        ))
-        ag[-1].start()
-    for d in range(1, n_mp):
-        rs[d - 1].wait_send()
-    for d in range(1, n_dp):
-        ag[d - 1].wait_recv()
-
-    every = ag_buf[...]
-    g_buf[mp] = lax.dot_general(
-        every, every, (((1,), (1,)), ((), ())), precision=HIGHEST, preferred_element_type=F32
-    )
-    gs = []
-    for d in range(1, n_mp):
-        peer = lax.rem(mp + d, n_mp)
-        gs.append(pltpu.make_async_remote_copy(
+        gs[d] = pltpu.make_async_remote_copy(
             src_ref=g_buf.at[mp], dst_ref=g_buf.at[mp], send_sem=g_send.at[d - 1],
             recv_sem=g_recv.at[d - 1], device_id=(dp, peer), device_id_type=MESH,
-        ))
-        gs[-1].start()
-    for d in range(1, n_dp):
-        ag[d - 1].wait_send()
-
+        )
+        gs[d].start()
+    for copy in list(rs.values()) + list(ag.values()):
+        copy.wait_send()
+    for d in range(1, n_mp):
+        gs[d].wait_recv()
+    gram = g_buf[0]
+    for p in range(1, n_mp):
+        gram = gram + g_buf[p]
+    gram_ref[...] = jnp.concatenate(
+        [gram[:, f * nseq : (f + 1) * nseq] for f in range(fold)], axis=0
+    )
+    for d in range(1, n_mp):
+        gs[d].wait_send()
+
+
+def score_kernel(dims, every_ref, gram_ref, ep_ref, cl_ref, fl_ref, lp_ref, pr_ref, d_buf):
+    slots, width, nseq, classes = dims
+    dp = lax.axis_index("dp")
+    own = pl.ds(pl.multiple_of(dp * slots, slots), slots)
+    every = every_ref[...]
+    gram = gram_ref[...]
     label = ep_ref[...] * WAYS + cl_ref[...]
     support = fl_ref[...] == 0
     class_row = lax.broadcasted_iota(jnp.int32, (classes, nseq), 0)
@@ -256,12 +303,6 @@
     mine = a == lax.broadcasted_iota(jnp.int32, (slots, nseq), 1)
     own_query = jnp.sum(jnp.where(mine, fl_ref[...].astype(F32), 0.0), axis=-1, keepdims=True)
     own_episode = jnp.sum(jnp.where(mine, ep_ref[...].astype(F32), 0.0), axis=-1, keepdims=True)
-
-    for d in range(1, n_mp):
-        gs[d - 1].wait_recv()
-    gram = g_buf[0]
-    for p in range(1, n_mp):
-        gram = gram + g_buf[p]
     eye = lax.broadcasted_iota(jnp.int32, (nseq, nseq), 0) == lax.broadcasted_iota(
         jnp.int32, (nseq, nseq), 1
     )
@@ -294,8 +335,6 @@
     shifted = logits - jnp.max(logits, axis=-1, keepdims=True)
     logp = shifted - jnp.log(jnp.sum(jnp.exp(shifted), axis=-1, keepdims=True))
     lp_ref[...] = jnp.where(own_query == 1.0, logp, 0.0)
-    for d in range(1, n_mp):
-        gs[d - 1].wait_send()
 
 
 def per_device(
@@ -328,8 +367,8 @@
         ),
         in_specs=[
             smem, smem,
-            pl.BlockSpec((tile, width), lambda i: (i, 0)),
-            pl.BlockSpec((1, width), lambda i: (0, 0)),
+            hbm,
+            vmem,
             hbm, hbm, hbm, hbm,
             pl.BlockSpec((tile, hd), lambda i: (i, 0)),
             pl.BlockSpec((tile, hd), lambda i: (i, 0)),
@@ -339,6 +378,9 @@
             pl.BlockSpec((slots, share), lambda i: (0, 0)),
         ),
         scratch_shapes=[
+            pltpu.VMEM((2, tile, width), BF16),
+            pltpu.VMEM((tile, (heads + 2) * hd), F32),
+            pltpu.VMEM((tile, 128), F32),
             pltpu.VMEM((width, (heads + 2) * hd), BF16),
             pltpu.VMEM(w_out.shape, BF16),
             pltpu.VMEM((heads, tile, hd), BF16),
@@ -348,39 +390,52 @@
             pltpu.VMEM((heads, rows, hd), F32),
             pltpu.SemaphoreType.DMA((width // chunk, 3)),
             pltpu.SemaphoreType.DMA,
+            pltpu.SemaphoreType.DMA((width // chunk,)),
+            pltpu.SemaphoreType.DMA((2,)),
         ],
         compiler_params=pltpu.CompilerParams(
             dimension_semantics=("arbitrary",), vmem_limit_bytes=60 * 1024 * 1024
         ),
     )(
-        seq_starts, seq_lengths, tokens, norm_gain.reshape(1, width),
+        seq_starts, seq_lengths, tokens, norm_gain,
         w_query, w_key, w_value, w_out, cos, sin,
     )
     nseq = episode_ids.shape[0]
     episodes = max(1, nseq // (2 * WAYS))
     classes = episodes * WAYS
-    dims = (n_dp, n_mp, slots, share, width, nseq, classes)
     dma = pltpu.SemaphoreType.DMA
+    pieces = 2 if share % 256 == 0 else 1
+    fold = 2 if nseq <= 64 else 1
+    dims = (n_dp, n_mp, slots, share, nseq, pieces, fold)
+    every, gram = pl.pallas_call(
+        functools.partial(exchange_kernel, dims),
+        out_shape=(
+            jax.ShapeDtypeStruct((nseq, share), F32),
+            jax.ShapeDtypeStruct((nseq, nseq), F32),
+        ),
+        in_specs=[vmem, vmem, smem],
+        out_specs=(vmem, vmem),
+        scratch_shapes=[
+            pltpu.VMEM((n_mp - 1, pieces, slots, share // pieces), F32),
+            pltpu.VMEM((pieces, nseq, share // pieces), F32),
+            pltpu.VMEM((n_mp, nseq // fold, nseq * fold), F32),
+            dma((pieces, n_mp - 1)), dma((pieces, n_mp - 1)),
+            dma((pieces, n_dp - 1)), dma((pieces, n_dp - 1)),
+            dma((n_mp - 1,)), dma((n_mp - 1,)),
+        ],
+        compiler_params=pltpu.CompilerParams(collective_id=0, has_side_effects=True),
+    )(head_part, token_sums, seq_lengths)
     return pl.pallas_call(
-        functools.partial(score_kernel, dims),
+        functools.partial(score_kernel, (slots, width, nseq, classes)),
         out_shape=(
             jax.ShapeDtypeStruct((slots, WAYS), F32),
             jax.ShapeDtypeStruct((classes, share), F32),
         ),
-        in_specs=[vmem, vmem, smem, vmem, vmem, vmem],
+        in_specs=[vmem] * 5,
         out_specs=(vmem, vmem),
-        scratch_shapes=[
-            pltpu.VMEM((n_mp - 1, slots, share), F32),
-            pltpu.VMEM((nseq, share), F32),
-            pltpu.VMEM((n_mp, nseq, nseq), F32),
-            pltpu.VMEM((nseq, nseq), F32),
-            dma((n_mp - 1,)), dma((n_mp - 1,)),
-            dma((n_dp - 1,)), dma((n_dp - 1,)),
-            dma((n_mp - 1,)), dma((n_mp - 1,)),
-        ],
-        compiler_params=pltpu.CompilerParams(collective_id=0, has_side_effects=True),
+        scratch_shapes=[pltpu.VMEM((nseq, nseq), F32)],
     )(
-        head_part, token_sums, seq_lengths,
+        every, gram,
         episode_ids.reshape(1, nseq), class_ids.reshape(1, nseq), query_flags.reshape(1, nseq),
     )
 

time: 54 us -> 53.7 us (level)
  local copies, waits for them, and re-layouts: 4.14 us -> 0 us
  Pallas kernels: 49.1 us -> 52.9 us
    pallas_call x1, Pallas kernels: 26.9 us -> 30.6 us  [per_device(): pl.pallas_call(functools.partial(encode_kernel, dims), grid=(rows // tile...]
    unnamed x2 -> x0, local copies, waits for them, and re-layouts: 2.83 us -> none
    reshape x1 -> x0, local copies, waits for them, and re-layouts: 1.31 us -> none  [per_device(): norm_gain.reshape(1, width)]
    pallas_call x1 -> x2, Pallas kernels: 22.2 us -> 22.3 us  [the longest x1 20.1 us: per_device(): pl.pallas_call(functools.partial(exchange_kernel, dims), out_shape=(jax.S...]
where the time goes in v2:
time: 53.7 us; the launch traced here: 53.5 us
  Pallas kernels  52.9 us (99%)
  between operations  0.65 us (1%)
    pallas_call x1, Pallas kernels, per_device(): pl.pallas_call(functools.partial(encode_kernel, dims), grid=(rows // tile...  30.6 us
    pallas_call x1, Pallas kernels, per_device(): pl.pallas_call(functools.partial(exchange_kernel, dims), out_shape=(jax.S...  20.1 us
    pallas_call x1, Pallas kernels, per_device(): pl.pallas_call(functools.partial(score_kernel, (slots, width, nseq, class...  2.12 us

profile of v2, /device:TPU:0, one launch (start us, length us, event | category | flops | bytes accessed | tf_op | source)
XLA Modules:
  0.0 53.5 jit_solution(8336622502286172264)
XLA Ops:
  0.6 30.6 %shard_map.140 = (f32[4,8,1024]{2,1,0:T(8,128)}, f32[8,1024]{1,0:T(8,128)}) custom-call(s32[8]{0:T(128)} %st_ref.1, s32[8]{0:T(128)} %ln_ref.3, bf16[1536,4096]{1,0:T(8,128)(2,1)} %x_hbm.1, bf16[4096]{0:T(1024)(128)(2,1)} %gain_ref.1, bf16[4096,512]{1,0:T(8,128)(2,1)} %wq_hbm.1, bf16[4096,128]{1,0:T(8,128)(2,1)} %wk_hbm.1, bf16[4096,128]{1,0:T(8,128)(2,1)} %wv_hbm.1, ...), custom_call_target="tpu_custom_call" | custom-call | tf_op jit(solution)/shard_map/pallas_call | solution.py:361
  31.3 20.1 %shard_map.141 = (f32[64,1024]{1,0:T(8,128)}, f32[64,64]{1,0:T(8,128)}) custom-call(f32[4,8,1024]{2,1,0:T(8,128)} %get-tuple-element.6.hp_ref, f32[8,1024]{1,0:T(8,128)} %get-tuple-element.7.ts_ref, s32[8]{0:T(128)} %ln_ref.3), custom_call_target="tpu_custom_call" | custom-call | tf_op jit(solution)/shard_map/pallas_call | solution.py:410
  51.4 2.1 %shard_map.142 = (f32[8,32]{1,0:T(8,128)}, f32[32,1024]{1,0:T(8,128)}) custom-call(f32[64,1024]{1,0:T(8,128)} %get-tuple-element.8.every_ref, f32[64,64]{1,0:T(8,128)} %get-tuple-element.9.gram_ref, s32[1,64]{1,0:T(1,128)} %bitcast.3, s32[1,64]{1,0:T(1,128)} %bitcast.4, s32[1,64]{1,0:T(1,128)} %bitcast.5), custom_call_target="tpu_custom_call" | custom-call | tf_op jit(solution)/shard_map/pallas_call | solution.py:428

commit v3 on v2

--- a/solution.py
+++ b/solution.py
@@ -27,8 +27,8 @@
 
 
 def encode_kernel(
-    dims, st_ref, ln_ref, x_hbm, gain_ref, wq_hbm, wk_hbm, wv_hbm, wo_hbm, cos_ref, sin_ref,
-    hp_ref, ts_ref, x_s, acc_s, sq_s, w_s, wo_s, q_s, k_s, v_s, s_s, c_s, w_sem, wo_sem, x0_sem, x_sem,
+    dims, st_ref, ln_ref, x_ref, gain_ref, wq_hbm, wk_hbm, wv_hbm, wo_hbm, cos_ref, sin_ref,
+    hp_ref, ts_ref, w_s, wo_s, q_s, k_s, v_s, s_s, c_s, w_sem, wo_sem,
 ):
     rows, tile, qb, width, slots, heads, chunk, share, n_mp = dims
     hd = HEAD_DIM
@@ -38,22 +38,6 @@
     chunks = width // chunk
     rank = lax.axis_index("mp")
     wo_copy = pltpu.make_async_copy(wo_hbm, wo_s, wo_sem)
-    now = lax.rem(i, 2)
-    x_ref = x_s.at[now]
-
-    def fetch(t, slot):
-        r = pl.ds(pl.multiple_of(t * tile, tile), tile)
-        return pltpu.make_async_copy(x_hbm.at[r, :], x_s.at[slot], x_sem.at[slot])
-
-    def squares(at, count, add):
-        half = tile // 2
-        for b in range(2):
-            r = slice(b * half, (b + 1) * half)
-            acc = sq_s[r, :] if add else jnp.zeros((half, 128), F32)
-            for v in range(at, at + count, 128):
-                x = x_ref[r, v : v + 128].astype(F32)
-                acc = acc + x * x
-            sq_s[r, :] = acc
 
     def members(first, count):
         slot = lax.broadcasted_iota(jnp.int32, (slots, count), 0)
@@ -70,7 +54,6 @@
         def copies(c):
             r = pl.ds(c * chunk, chunk)
             return (
-                pltpu.make_async_copy(x_hbm.at[pl.ds(0, tile), r], x_s.at[0, :, r], x0_sem.at[c]),
                 pltpu.make_async_copy(wq_hbm.at[r, :], w_s.at[r, pl.ds(0, q_cols)], w_sem.at[c, 0]),
                 pltpu.make_async_copy(wk_hbm.at[r, :], w_s.at[r, pl.ds(q_cols, hd)], w_sem.at[c, 1]),
                 pltpu.make_async_copy(wv_hbm.at[r, :], w_s.at[r, pl.ds(q_cols + hd, hd)], w_sem.at[c, 2]),
@@ -79,8 +62,6 @@
         for c in range(chunks):
             for copy in copies(c):
                 copy.start()
-        if rows > tile:
-            fetch(1, 1).start()
         wo_copy.start()
         ts_ref[...] = jnp.zeros_like(ts_ref)
         c_s[...] = jnp.zeros_like(c_s)
@@ -93,24 +74,17 @@
                 for v in range(heads + 2):
                     w = w_s[at : at + 128, v * hd : (v + 1) * hd].astype(F32)
                     w_s[at : at + 128, v * hd : (v + 1) * hd] = (w * g).astype(BF16)
-            r = slice(c * chunk, (c + 1) * chunk)
-            part = jnp.dot(x_s[0, :, r], w_s[r, :], preferred_element_type=F32)
-            acc_s[...] = part if c == 0 else acc_s[...] + part
-            squares(c * chunk, chunk, c > 0)
-
-    @pl.when(i > 0)
-    def _():
-        fetch(i, now).wait()
-
-        @pl.when(i < last)
-        def _():
-            fetch(i + 1, 1 - now).start()
-
-        acc_s[...] = jnp.dot(x_ref[...], w_s[...], preferred_element_type=F32)
-        squares(0, width, False)
-
-    rstd = lax.rsqrt(jnp.sum(sq_s[...], axis=-1, keepdims=True) / width + 1e-05)
-    proj = acc_s
+
+    half = tile // 2
+    sums = []
+    for b in range(2):
+        acc = jnp.zeros((half, 128), F32)
+        for v in range(width // 128):
+            x = x_ref[b * half : (b + 1) * half, v * 128 : (v + 1) * 128].astype(F32)
+            acc = acc + x * x
+        sums.append(jnp.sum(acc, axis=-1, keepdims=True))
+    rstd = lax.rsqrt(jnp.concatenate(sums, axis=0) / width + 1e-05)
+    proj = jnp.dot(x_ref[...], w_s[...], preferred_element_type=F32)
     cos = cos_ref[...]
     sin = sin_ref[...]
 
@@ -122,7 +96,7 @@
         q_s[h] = rope(proj[:, h * hd : (h + 1) * hd] * q_rstd)
     here = pl.ds(pl.multiple_of(i * tile, tile), tile)
     k_s[here, :] = rope(proj[:, q_cols : q_cols + hd] * rstd)
-    v_s[here, :] = (proj[:, q_cols + hd : q_cols + 2 * hd] * rstd).astype(BF16)
+    v_s[here, :] = (proj[:, q_cols + hd :] * rstd).astype(BF16)
     cols = pl.ds(pl.multiple_of(rank * share, share), share)
     ts_ref[...] += jnp.dot(members(i * tile, tile), x_ref[:, cols], preferred_element_type=F32)
 
@@ -196,7 +170,12 @@
         for h in range(heads):
             mass = jnp.sum(c_s[h], axis=-1, keepdims=True)
             mixed = mass * v_s[...].astype(F32)
-            parts.append(jnp.dot(member, mixed.astype(BF16), preferred_element_type=F32))
+            high = mixed.astype(BF16)
+            low = (mixed - high.astype(F32)).astype(BF16)
+            parts.append(
+                jnp.dot(member, high, preferred_element_type=F32)
+                + jnp.dot(member, low, preferred_element_type=F32)
+            )
         attended = jnp.concatenate(parts, axis=-1)
         high = attended.astype(BF16)
         low = attended - high.astype(F32)
@@ -367,7 +346,7 @@
         ),
         in_specs=[
             smem, smem,
-            hbm,
+            pl.BlockSpec((tile, width), lambda i: (i, 0)),
             vmem,
             hbm, hbm, hbm, hbm,
             pl.BlockSpec((tile, hd), lambda i: (i, 0)),
@@ -378,9 +357,6 @@
             pl.BlockSpec((slots, share), lambda i: (0, 0)),
         ),
         scratch_shapes=[
-            pltpu.VMEM((2, tile, width), BF16),
-            pltpu.VMEM((tile, (heads + 2) * hd), F32),
-            pltpu.VMEM((tile, 128), F32),
             pltpu.VMEM((width, (heads + 2) * hd), BF16),
             pltpu.VMEM(w_out.shape, BF16),
             pltpu.VMEM((heads, tile, hd), BF16),
@@ -390,8 +366,6 @@
             pltpu.VMEM((heads, rows, hd), F32),
             pltpu.SemaphoreType.DMA((width // chunk, 3)),
             pltpu.SemaphoreType.DMA,
-            pltpu.SemaphoreType.DMA((width // chunk,)),
-            pltpu.SemaphoreType.DMA((2,)),
         ],
         compiler_params=pltpu.CompilerParams(
             dimension_semantics=("arbitrary",), vmem_limit_bytes=60 * 1024 * 1024

time: 53.7 us -> 50.2 us (0.935)
  Pallas kernels: 52.9 us -> 49.7 us
    pallas_call x1, Pallas kernels: 30.6 us -> 27.5 us  [per_device(): pl.pallas_call(functools.partial(encode_kernel, dims), grid=(rows // tile...]
where the time goes in v3:
time: 50.2 us; the launch traced here: 50.3 us
  Pallas kernels  49.7 us (99%)
  between operations  0.65 us (1%)
    pallas_call x1, Pallas kernels, per_device(): pl.pallas_call(functools.partial(encode_kernel, dims), grid=(rows // tile...  27.5 us
    pallas_call x1, Pallas kernels, per_device(): pl.pallas_call(functools.partial(exchange_kernel, dims), out_shape=(jax.S...  20.1 us
    pallas_call x1, Pallas kernels, per_device(): pl.pallas_call(functools.partial(score_kernel, (slots, width, nseq, class...  2.12 us

profile of v3, /device:TPU:0, one launch (start us, length us, event | category | flops | bytes accessed | tf_op | source)
XLA Modules:
  0.0 50.3 jit_solution(7118973296975335454)
XLA Ops:
  0.6 27.5 %shard_map.140 = (f32[4,8,1024]{2,1,0:T(8,128)}, f32[8,1024]{1,0:T(8,128)}) custom-call(s32[8]{0:T(128)} %st_ref.1, s32[8]{0:T(128)} %ln_ref.3, bf16[1536,4096]{1,0:T(8,128)(2,1)} %x_ref.1, bf16[4096]{0:T(1024)(128)(2,1)} %gain_ref.1, bf16[4096,512]{1,0:T(8,128)(2,1)} %wq_hbm.1, bf16[4096,128]{1,0:T(8,128)(2,1)} %wk_hbm.1, bf16[4096,128]{1,0:T(8,128)(2,1)} %wv_hbm.1, ...), custom_call_target="tpu_custom_call" | custom-call | tf_op jit(solution)/shard_map/pallas_call | solution.py:340
  28.1 20.1 %shard_map.141 = (f32[64,1024]{1,0:T(8,128)}, f32[64,64]{1,0:T(8,128)}) custom-call(f32[4,8,1024]{2,1,0:T(8,128)} %get-tuple-element.6.hp_ref, f32[8,1024]{1,0:T(8,128)} %get-tuple-element.7.ts_ref, s32[8]{0:T(128)} %ln_ref.3), custom_call_target="tpu_custom_call" | custom-call | tf_op jit(solution)/shard_map/pallas_call | solution.py:384
  48.2 2.1 %shard_map.142 = (f32[8,32]{1,0:T(8,128)}, f32[32,1024]{1,0:T(8,128)}) custom-call(f32[64,1024]{1,0:T(8,128)} %get-tuple-element.8.every_ref, f32[64,64]{1,0:T(8,128)} %get-tuple-element.9.gram_ref, s32[1,64]{1,0:T(1,128)} %bitcast.3, s32[1,64]{1,0:T(1,128)} %bitcast.4, s32[1,64]{1,0:T(1,128)} %bitcast.5), custom_call_target="tpu_custom_call" | custom-call | tf_op jit(solution)/shard_map/pallas_call | solution.py:402
